TPU v7x, 32 devices: a whole 2x2x4 slice. The times are simulated.
32 devices in a mesh: inst: 4 (over x, core), blk: 8 (over z, y).
Axes of the slice: x: 2, y: 2, z: 4, core: 2. Of those that a mesh axis runs over, the one named last changes fastest.
Arguments:
- state: float32 [16, 5, 16, 64, 256], P('inst', None, None, 'blk'), may hold values from -0.53 to 3.9, as said below
- multiples: int32 [7], replicated, may hold values from 1 to 4
Outputs:
- state_change: float32 [16, 5, 16, 64, 256], P('inst', None, None, 'blk')
Inputs may be any that keep to these rules, and one draw needn't show every extreme that they name: `state`: density and pressure lie in 0.7 to 1.3, the axial velocity in 0.2 to 0.8 and the other two velocity components in -0.4 to 0.4; the last variable is the total energy p / 0.4 + rho (u u + v v + w w) / 2.
All inputs are finite; a program needn't handle non-finite values.
Results may differ from a plain program's by a relative error of at most 0.0003.
Values sent between devices are 32-bit elements; how exact they have to be, the bound alone decides.
No kernel may reach another device: no remote copies, remote signals or barrier semaphores. Data moves between devices by JAX's collectives and lax.ppermute only.
A program may use at most 128 MiB of HBM per device.

v0:
```python
import math
import jax
import jax.numpy as jnp
from jax import lax
from jax.sharding import PartitionSpec as P

NT = 16
heat_ratio = 1.4
segment_step = 0.05
smooth_weight = 0.5
base_rate = 0.5
diagonal_weight = 3.0


def extended_2(cells, sides, width):
    for axis, dim in sides:
        count = lax.axis_size(axis)
        head = lax.slice_in_dim(cells, 0, width, axis=dim)
        tail = lax.slice_in_dim(cells, cells.shape[dim] - width, cells.shape[dim], axis=dim)
        cells = jnp.concatenate(
            [
                lax.ppermute(tail, axis, [(i, (i + 1) % count) for i in range(count)]),
                cells,
                lax.ppermute(head, axis, [((i + 1) % count, i) for i in range(count)]),
            ],
            axis=dim,
        )
    return cells


def limited(lower, upper):
    return jnp.maximum(0.0, jnp.minimum(lower, upper)) + jnp.minimum(0.0, jnp.maximum(lower, upper))


def take_part(array_in, offset, amount, along):
    return lax.slice_in_dim(array_in, offset, offset + amount, axis=along)


def primitive(conserved):
    density = conserved[:, 0]
    velocity = [conserved[:, 1] / density, conserved[:, 2] / density, conserved[:, 3] / density]
    kinetic = (
        0.5
        * density
        * (velocity[0] * velocity[0] + velocity[1] * velocity[1] + velocity[2] * velocity[2])
    )
    pressure = (heat_ratio - 1.0) * (conserved[:, 4] - kinetic)
    return [density] + velocity + [pressure]


def physical(states, normal):
    density = states[0]
    pressure = states[4]
    velocity = states[1:4]
    normal_speed = velocity[normal]
    energy = pressure / (heat_ratio - 1.0) + 0.5 * density * (
        velocity[0] * velocity[0] + velocity[1] * velocity[1] + velocity[2] * velocity[2]
    )
    conserved = [
        density,
        density * velocity[0],
        density * velocity[1],
        density * velocity[2],
        energy,
    ]
    flux = [density * normal_speed]
    for member in range(3):
        momentum = density * normal_speed * velocity[member]
        if member == normal:
            momentum = momentum + pressure
        flux.append(momentum)
    flux.append((energy + pressure) * normal_speed)
    wave_speed = jnp.abs(normal_speed) + jnp.sqrt(heat_ratio * pressure / density)
    return (flux, conserved, wave_speed)


def divergence(states, along, normal):
    extent = states[0].shape[along]
    interior = extent - 4
    left_side = []
    right_side = []
    for component in states:
        differences = take_part(component, 1, extent - 1, along) - take_part(
            component, 0, extent - 1, along
        )
        slopes = limited(
            take_part(differences, 0, interior + 2, along),
            take_part(differences, 1, interior + 2, along),
        )
        centres = take_part(component, 1, interior + 2, along)
        left_side.append(
            take_part(centres, 0, interior + 1, along)
            + 0.5 * take_part(slopes, 0, interior + 1, along)
        )
        right_side.append(
            take_part(centres, 1, interior + 1, along)
            - 0.5 * take_part(slopes, 1, interior + 1, along)
        )
    left_flux, left_cons, left_speed = physical(left_side, normal)
    right_flux, right_cons, right_speed = physical(right_side, normal)
    wave_speed = jnp.maximum(left_speed, right_speed)
    result = []
    for member in range(5):
        face_flux = 0.5 * (left_flux[member] + right_flux[member]) - 0.5 * wave_speed * (
            right_cons[member] - left_cons[member]
        )
        result.append(
            take_part(face_flux, 1, interior, along) - take_part(face_flux, 0, interior, along)
        )
    return result


def residual(extended):
    states = primitive(extended)
    inner = [component[:, :, 2:-2, :] for component in states]
    circum = divergence(states, 2, 1)
    axial = divergence(
        [jnp.pad(component, ((0, 0), (2, 2), (0, 0), (0, 0)), mode="edge") for component in inner],
        1,
        0,
    )
    radial = divergence(
        [jnp.pad(component, ((0, 0), (0, 0), (0, 0), (2, 2)), mode="edge") for component in inner],
        3,
        2,
    )
    return jnp.stack(
        [axial[member] + circum[member] + radial[member] for member in range(5)], axis=1
    )


def transform_tables(instances):
    indices = jnp.arange(instances, dtype=jnp.int32)
    harmonic = jnp.where(indices < 2, indices * (instances // 2), indices // 2)
    phases = harmonic[:, None] * indices[None, :] % instances
    angles = phases.astype(jnp.float32) * (2.0 * math.pi / instances)
    sine_rows = (indices % 2 == 1) & (indices >= 2)
    basis = jnp.where(sine_rows[:, None], jnp.sin(angles), jnp.cos(angles))
    weights = jnp.where(indices < 2, 1.0 / instances, 2.0 / instances).astype(jnp.float32)
    return (basis * weights[:, None], basis.T)


def pair_solve(right, frequency):
    cosine_part = right[:, 0]
    sine_part = right[:, 1]
    determinant = diagonal_weight * diagonal_weight + frequency * frequency
    return jnp.stack(
        [
            (diagonal_weight * cosine_part - frequency * sine_part) / determinant,
            (diagonal_weight * sine_part + frequency * cosine_part) / determinant,
        ],
        axis=1,
    )


def neighbours(extended):
    circum = extended[:, :, :, :, :-2] + extended[:, :, :, :, 2:]
    middle = extended[:, :, :, :, 1:-1]
    padded = jnp.pad(middle, ((0, 0), (0, 0), (0, 0), (0, 0), (0, 0), (1, 1)))
    return circum + (padded[:, :, :, :, :, :-2] + padded[:, :, :, :, :, 2:])


def body(state, multiples):
    extended = extended_2(state, (("blk", 3),), 2)
    first_sweep = residual(extended)
    segmented = state - segment_step * first_sweep
    segmented_ext = extended_2(segmented, (("blk", 3),), 2)
    second_sweep = residual(segmented_ext)
    state_freq, residual_freq = (
        lax.all_to_all(state, "inst", split_axis=2, concat_axis=0, tiled=True),
        lax.all_to_all(second_sweep, "inst", split_axis=2, concat_axis=0, tiled=True),
    )
    forward, inverse = transform_tables(NT)
    layout = residual_freq.shape
    paired = (NT // 2, 2) + layout[1:]
    residual_hat = jnp.dot(
        forward, residual_freq.reshape(NT, -1), precision=lax.Precision.HIGHEST
    ).reshape(paired)
    state_hat = jnp.dot(
        forward, state_freq.reshape(NT, -1), precision=lax.Precision.HIGHEST
    ).reshape(paired)
    frequency = jnp.concatenate(
        [jnp.zeros((1,), jnp.float32), base_rate * multiples.astype(jnp.float32)]
    ).reshape(NT // 2, 1, 1, 1, 1)
    source = jnp.stack([frequency * state_hat[:, 1], -frequency * state_hat[:, 0]], axis=1)
    right_hand = -(residual_hat + source)
    widened = extended_2(right_hand, (("blk", 4),), 3)
    correction = pair_solve(widened, frequency)
    for repeat in range(3):
        trimmed = lax.slice_in_dim(widened, repeat + 1, widened.shape[4] - repeat - 1, axis=4)
        correction = pair_solve(trimmed + smooth_weight * neighbours(correction), frequency)
    change_freq = jnp.dot(
        inverse, correction.reshape(NT, -1), precision=lax.Precision.HIGHEST
    ).reshape(layout)
    return lax.all_to_all(change_freq, "inst", split_axis=0, concat_axis=2, tiled=True)


def solution(mesh):
    return jax.shard_map(
        body,
        mesh=mesh,
        in_specs=(P("inst", None, None, "blk", None), P()),
        out_specs=P("inst", None, None, "blk", None),
        check_vma=False,
    )
```

profile of v0, /device:TPU:0, one launch (start us, length us, event | category | flops | bytes accessed | tf_op | source)
XLA Modules:
  0.0 393.5 jit_solution(17723114507473512996)
XLA Ops:
  0.0 3.2 fusion.217
  3.2 3.0 collective-permute-start
  6.2 3.1 collective-permute-start.1
  9.3 24.9 %collective-permute-done = f32[4,5,16,2,256]{4,3,0,2,1:T(2,128)S(1)} collective-permute-done((f32[4,5,16,2,256]{4,3,0,2,1:T(2,128)S(1)}, f32[4,5,16,2,256]{4,3,0,2,1:T(2,128)S(1)}, u32[]{:S(2)}, u32[]{:S(2)}) %collective-permute-start) | collective-permute-done | bytes 655392 | tf_op jit(solution)/shard_map/ppermute | solution.py:22
  94.3 4.1 %multiply_subtract_fusion.16 = (f32[4,16,8,257]{3,2,0,1:T(8,128)S(1)}, f32[4,16,8,257]{3,2,0,1:T(8,128)S(1)}, f32[4,16,8,257]{3,2,0,1:T(8,128)S(1)}, f32[4,16,8,257]{3,2,0,1:T(8,128)S(1)}, f32[4,16,8,257]{3,2,0,1:T(8,128)S(1)}) fusion(f32[4,16,8,258]{3,2,0,1:T(8,128)S(1)} %copy-done.26, f32[4,16,8,256]{3,2,0,1:T(8,128)S(1)} %copy-done.34, ...), kind=kLoop, calls=%fused_computation.254 | loop fusion | flops 8816128 | bytes 10557440 | tf_op jit(solution)/shard_map/sub | solution.py:104
  107.6 3.5 multiply_subtract_fusion.6
  119.5 4.4 %collective-permute-start.3 = (f32[4,5,16,2,256]{4,3,0,2,1:T(2,128)}, f32[4,5,16,2,256]{4,3,0,2,1:T(2,128)}, u32[]{:S(2)}, u32[]{:S(2)}) collective-permute-start(f32[4,5,16,2,256]{4,3,0,2,1:T(2,128)} %get-tuple-element.74), channel_id=1, source_target_pairs={{1,0},{2,1},{3,2},{4,3},{5,4},{6,5},{7,6},{0,7},{9,8},{10,9},{11,1... | collective-permute-start | bytes 1966088 | tf_op jit(solution)/shard_map/ppermute | solution.py:24
  125.7 4.5 %all-to-all-start.1 = ((f32[4,5,16,8,256]{4,3,1,0,2:T(8,128)}), f32[4,5,16,8,256]{4,3,1,0,2:T(8,128)}, u32[]{:S(2)}, u32[]{:S(2)}) async-start(f32[4,5,16,8,256]{4,3,1,0,2:T(8,128)} %copy.120), calls=%async_computation.1 | async-start | bytes 5242880 | tf_op jit(solution)/shard_map/all_to_all | solution.py:170
  130.3 16.7 %collective-permute-done.2 = f32[4,5,16,2,256]{4,3,0,2,1:T(2,128)S(1)} collective-permute-done((f32[4,5,16,2,256]{4,3,0,2,1:T(2,128)}, f32[4,5,16,2,256]{4,3,0,2,1:T(2,128)S(1)}, u32[]{:S(2)}, u32[]{:S(2)}) %collective-permute-start.2) | collective-permute-done | bytes 655392 | tf_op jit(solution)/shard_map/ppermute | solution.py:22
  147.0 3.9 collective-permute-done.3
  217.7 4.0 %multiply_subtract_fusion.11 = (f32[4,16,8,257]{3,2,0,1:T(8,128)S(1)}, f32[4,16,8,257]{3,2,0,1:T(8,128)S(1)}, f32[4,16,8,257]{3,2,0,1:T(8,128)S(1)}, f32[4,16,8,257]{3,2,0,1:T(8,128)S(1)}, f32[4,16,8,257]{3,2,0,1:T(8,128)S(1)}) fusion(f32[4,16,8,258]{3,2,0,1:T(8,128)S(1)} %minimum_add_fusion.11, f32[4,16,8,256]{3,2,0,1:T(8,128)S(1)} %copy-done.32, ...), kind=kLoop, calls=%fused_computation.243 | loop fusion | flops 8816128 | bytes 10557440 | tf_op jit(solution)/shard_map/sub | solution.py:104
  228.7 4.3 %multiply_subtract_fusion.1 = (f32[4,16,9,256]{3,2,0,1:T(8,128)S(1)}, f32[4,16,9,256]{3,2,0,1:T(8,128)S(1)}, f32[4,16,9,256]{3,2,0,1:T(8,128)S(1)}, f32[4,16,9,2...) fusion(f32[4,16,10,256]{3,2,0,1:T(8,128)S(1)} %minimum_add_fusion.1, ...), kind=kLoop, calls=%fused_computation.141 | loop fusion | flops 8404992 | bytes 15335424 | tf_op jit(solution)/shard_map/sub | solution.py:104
  233.0 3.3 multiply_subtract_fusion.2
  244.7 4.0 %all-to-all-start = ((f32[4,5,16,8,256]{4,3,0,1,2:T(8,128)}), f32[4,5,16,8,256]{4,3,0,1,2:T(8,128)S(1)}, u32[]{:S(2)}, u32[]{:S(2)}) async-start(f32[4,5,16,8,256]{4,3,0,1,2:T(8,128)} %copy.116), calls=%async_computation | async-start | bytes 5242880 | tf_op jit(solution)/shard_map/all_to_all | solution.py:171
  248.9 3.6 copy.151
  252.5 3.1 reshape.409
  258.1 3.7 fusion.22
  263.8 16.2 %all-to-all-done = f32[4,5,16,8,256]{4,3,0,1,2:T(8,128)S(1)} async-done(((f32[4,5,16,8,256]{4,3,0,1,2:T(8,128)}), f32[4,5,16,8,256]{4,3,0,1,2:T(8,128)S(1)}, u32[]{:S(2)}, u32[]{:S(2)}) %all-to-all-start) | async-done | bytes 2621472 | tf_op jit(solution)/shard_map/all_to_all | solution.py:171
  285.5 3.9 fusion.21
  289.8 5.1 %collective-permute-start.5 = (f32[8,2,5,4,3,256]{5,0,4,3,2,1:T(8,128)S(1)}, f32[8,2,5,4,3,256]{5,0,4,3,2,1:T(8,128)S(1)}, u32[]{:S(2)}, u32[]{:S(2)}) collective-permute-start(f32[8,2,5,4,3,256]{5,0,4,3,2,1:T(8,128)S(1)} %get-tuple-element.72), channel_id=1, source_target_pairs={{1,0},{2,1},{3,2},{4,3},{5,4},{6,5},{7,6},{0,7},{9,8},{10,9},{11,1... | collective-permute-start | bytes 2949128 | tf_op jit(solution)/shard_map/ppermute | solution.py:24
  294.9 36.9 %collective-permute-done.4 = f32[8,2,5,4,3,256]{5,0,4,3,2,1:T(8,128)S(1)} collective-permute-done((f32[8,2,5,4,3,256]{5,0,4,3,2,1:T(8,128)S(1)}, f32[8,2,5,4,3,256]{5,0,4,3,2,1:T(8,128)S(1)}, u32[]{:S(2)}, u32[]{:S(2)}) %collective-permute-start.4) | collective-permute-done | bytes 983072 | tf_op jit(solution)/shard_map/ppermute | solution.py:22
  331.8 3.5 collective-permute-done.5
  352.6 3.6 fusion.26
  357.8 33.8 %all_to_all.48 = f32[16,5,4,8,256]{4,3,2,1,0:T(8,128)S(1)} all-to-all(f32[16,5,4,8,256]{4,3,2,1,0:T(8,128)S(1)} %copy.125), channel_id=1, replica_groups=mesh['inst'=4,'blk'=8] {'inst'}, dimensions={0} | all-to-all | bytes 5242880 | tf_op jit(solution)/shard_map/all_to_all | solution.py:195
  (462 shorter events, 190.5 us)
Async XLA Ops:
  0.0 36.5 %copy-start.18 = (f32[4,5,16,8,256]{4,3,2,1,0:T(8,128)S(1)}, f32[4,5,16,8,256]{4,3,2,1,0:T(8,128)}, u32[]{:S(2)}) copy-start(f32[4,5,16,8,256]{4,3,2,1,0:T(8,128)} %param.2) | copy-start | bytes 7864324
  3.2 31.1 %collective-permute-start = (f32[4,5,16,2,256]{4,3,0,2,1:T(2,128)S(1)}, f32[4,5,16,2,256]{4,3,0,2,1:T(2,128)S(1)}, u32[]{:S(2)}, u32[]{:S(2)}) collective-permute-start(f32[4,5,16,2,256]{4,3,0,2,1:T(2,128)S(1)} %get-tuple-element.75), channel_id=1, source_target_pairs={{0,1},{1,2},{2,3},{3,4},{4,5},{5,6},{6,7},{7,0},{8,9},{9,10},{10,1... | collective-permute-start | bytes 1966088 | tf_op jit(solution)/shard_map/ppermute | solution.py:22
  6.2 30.2 %collective-permute-start.1 = (f32[4,5,16,2,256]{4,3,0,2,1:T(2,128)S(1)}, f32[4,5,16,2,256]{4,3,0,2,1:T(2,128)S(1)}, u32[]{:S(2)}, u32[]{:S(2)}) collective-permute-start(f32[4,5,16,2,256]{4,3,0,2,1:T(2,128)S(1)} %get-tuple-element.76), channel_id=1, source_target_pairs={{1,0},{2,1},{3,2},{4,3},{5,4},{6,5},{7,6},{0,7},{9,8},{10,9},{11,1... | collective-permute-start | bytes 1966088 | tf_op jit(solution)/shard_map/ppermute | solution.py:24
  38.3 9.3 %copy-start.10 = (f32[4,16,12,256]{3,2,0,1:T(8,128)}, f32[4,16,12,256]{3,2,0,1:T(8,128)S(1)}, u32[]{:S(2)}) copy-start(f32[4,16,12,256]{3,2,0,1:T(8,128)S(1)} %get-tuple-element.45) | copy-start | bytes 2359300
  38.4 4.8 %copy-start.29 = (f32[4,16,8,256]{3,2,0,1:T(8,128)}, f32[4,16,8,256]{3,2,0,1:T(8,128)S(1)}, u32[]{:S(2)}) copy-start(f32[4,16,8,256]{3,2,0,1:T(8,128)S(1)} %slice.1936) | copy-start | bytes 1572868
  38.5 6.3 %copy-start.22 = (f32[4,16,8,256]{3,2,0,1:T(8,128)}, f32[4,16,8,256]{3,2,0,1:T(8,128)S(1)}, u32[]{:S(2)}) copy-start(f32[4,16,8,256]{3,2,0,1:T(8,128)S(1)} %slice.1978) | copy-start | bytes 1572868
  38.6 6.2 %copy-start.4 = (f32[4,16,8,256]{3,2,0,1:T(8,128)}, f32[4,16,8,256]{3,2,0,1:T(8,128)S(1)}, u32[]{:S(2)}) copy-start(f32[4,16,8,256]{3,2,0,1:T(8,128)S(1)} %slice.1892) | copy-start | bytes 1572868
  38.9 10.0 %copy-start.14 = (f32[4,16,12,256]{3,2,0,1:T(8,128)}, f32[4,16,12,256]{3,2,0,1:T(8,128)S(1)}, u32[]{:S(2)}) copy-start(f32[4,16,12,256]{3,2,0,1:T(8,128)S(1)} %slice_bitcast_fusion.9) | copy-start | bytes 2359300
  39.2 5.6 %copy-start.8 = (f32[4,18,8,256]{3,2,0,1:T(8,128)}, f32[4,18,8,256]{3,2,0,1:T(8,128)S(1)}, u32[]{:S(2)}) copy-start(f32[4,18,8,256]{3,2,0,1:T(8,128)S(1)} %minimum_add_fusion.27) | copy-start | bytes 1769476
  119.2 27.8 %collective-permute-start.2 = (f32[4,5,16,2,256]{4,3,0,2,1:T(2,128)}, f32[4,5,16,2,256]{4,3,0,2,1:T(2,128)S(1)}, u32[]{:S(2)}, u32[]{:S(2)}) collective-permute-start(f32[4,5,16,2,256]{4,3,0,2,1:T(2,128)} %get-tuple-element.73), channel_id=1, source_target_pairs={{0,1},{1,2},{2,3},{3,4},{4,5},{5,6},{6,7},{7,0},{8,9},{9,10},{10,1... | collective-permute-start | bytes 1966088 | tf_op jit(solution)/shard_map/ppermute | solution.py:22
  119.5 31.4 %collective-permute-start.3 = (f32[4,5,16,2,256]{4,3,0,2,1:T(2,128)}, f32[4,5,16,2,256]{4,3,0,2,1:T(2,128)}, u32[]{:S(2)}, u32[]{:S(2)}) collective-permute-start(f32[4,5,16,2,256]{4,3,0,2,1:T(2,128)} %get-tuple-element.74), channel_id=1, source_target_pairs={{1,0},{2,1},{3,2},{4,3},{5,4},{6,5},{7,6},{0,7},{9,8},{10,9},{11,1... | collective-permute-start | bytes 1966088 | tf_op jit(solution)/shard_map/ppermute | solution.py:24
  125.7 119.0 %all-to-all-start.1 = ((f32[4,5,16,8,256]{4,3,1,0,2:T(8,128)}), f32[4,5,16,8,256]{4,3,1,0,2:T(8,128)}, u32[]{:S(2)}, u32[]{:S(2)}) async-start(f32[4,5,16,8,256]{4,3,1,0,2:T(8,128)} %copy.120), calls=%async_computation.1 | async-start | bytes 5242880 | tf_op jit(solution)/shard_map/all_to_all | solution.py:170
  153.2 18.8 %copy-start.16 = (f32[4,16,12,256]{3,2,0,1:T(8,128)}, f32[4,16,12,256]{3,2,0,1:T(8,128)S(1)}, u32[]{:S(2)}) copy-start(f32[4,16,12,256]{3,2,0,1:T(8,128)S(1)} %slice_bitcast_fusion.4) | copy-start | bytes 2359300
  153.3 7.6 %copy-start.37 = (f32[4,16,8,256]{3,2,0,1:T(8,128)}, f32[4,16,8,256]{3,2,0,1:T(8,128)S(1)}, u32[]{:S(2)}) copy-start(f32[4,16,8,256]{3,2,0,1:T(8,128)S(1)} %slice.2032) | copy-start | bytes 1572868
  154.2 16.7 %copy-start.12 = (f32[4,16,12,256]{3,2,0,1:T(8,128)}, f32[4,16,12,256]{3,2,0,1:T(8,128)S(1)}, u32[]{:S(2)}) copy-start(f32[4,16,12,256]{3,2,0,1:T(8,128)S(1)} %get-tuple-element.25) | copy-start | bytes 2359300
  154.3 6.6 %copy-start.31 = (f32[4,16,8,256]{3,2,0,1:T(8,128)}, f32[4,16,8,256]{3,2,0,1:T(8,128)S(1)}, u32[]{:S(2)}) copy-start(f32[4,16,8,256]{3,2,0,1:T(8,128)S(1)} %slice.2041) | copy-start | bytes 1572868
  154.4 11.0 %copy-start.2 = (f32[4,16,8,256]{3,2,0,1:T(8,128)}, f32[4,16,8,256]{3,2,0,1:T(8,128)S(1)}, u32[]{:S(2)}) copy-start(f32[4,16,8,256]{3,2,0,1:T(8,128)S(1)} %slice.2054) | copy-start | bytes 1572868
  154.5 6.4 %copy-start.27 = (f32[4,16,8,256]{3,2,0,1:T(8,128)}, f32[4,16,8,256]{3,2,0,1:T(8,128)S(1)}, u32[]{:S(2)}) copy-start(f32[4,16,8,256]{3,2,0,1:T(8,128)S(1)} %slice.2098) | copy-start | bytes 1572868
  154.6 9.2 %copy-start.20 = (f32[4,16,8,256]{3,2,0,1:T(8,128)}, f32[4,16,8,256]{3,2,0,1:T(8,128)S(1)}, u32[]{:S(2)}) copy-start(f32[4,16,8,256]{3,2,0,1:T(8,128)S(1)} %slice.2140) | copy-start | bytes 1572868
  160.3 5.1 %copy-start.6 = (f32[4,18,8,256]{3,2,0,1:T(8,128)}, f32[4,18,8,256]{3,2,0,1:T(8,128)S(1)}, u32[]{:S(2)}) copy-start(f32[4,18,8,256]{3,2,0,1:T(8,128)S(1)} %minimum_add_fusion.22) | copy-start | bytes 1769476
  176.9 4.5 %copy-start.90 = (f32[4,16,8,2]{3,2,0,1:T(8,128)}, f32[4,16,8,2]{3,2,0,1:T(8,128)S(1)}, u32[]{:S(2)}) copy-start(f32[4,16,8,2]{3,2,0,1:T(8,128)S(1)} %reshape.394) | copy-start | bytes 12292
  244.7 35.2 %all-to-all-start = ((f32[4,5,16,8,256]{4,3,0,1,2:T(8,128)}), f32[4,5,16,8,256]{4,3,0,1,2:T(8,128)S(1)}, u32[]{:S(2)}, u32[]{:S(2)}) async-start(f32[4,5,16,8,256]{4,3,0,1,2:T(8,128)} %copy.116), calls=%async_computation | async-start | bytes 5242880 | tf_op jit(solution)/shard_map/all_to_all | solution.py:171
  289.7 42.1 %collective-permute-start.4 = (f32[8,2,5,4,3,256]{5,0,4,3,2,1:T(8,128)S(1)}, f32[8,2,5,4,3,256]{5,0,4,3,2,1:T(8,128)S(1)}, u32[]{:S(2)}, u32[]{:S(2)}) collective-permute-start(f32[8,2,5,4,3,256]{5,0,4,3,2,1:T(8,128)S(1)} %get-tuple-element.71), channel_id=1, source_target_pairs={{0,1},{1,2},{2,3},{3,4},{4,5},{5,6},{6,7},{7,0},{8,9},{9,10},{10,1... | collective-permute-start | bytes 2949128 | tf_op jit(solution)/shard_map/ppermute | solution.py:22
  289.8 45.5 %collective-permute-start.5 = (f32[8,2,5,4,3,256]{5,0,4,3,2,1:T(8,128)S(1)}, f32[8,2,5,4,3,256]{5,0,4,3,2,1:T(8,128)S(1)}, u32[]{:S(2)}, u32[]{:S(2)}) collective-permute-start(f32[8,2,5,4,3,256]{5,0,4,3,2,1:T(8,128)S(1)} %get-tuple-element.72), channel_id=1, source_target_pairs={{1,0},{2,1},{3,2},{4,3},{5,4},{6,5},{7,6},{0,7},{9,8},{10,9},{11,1... | collective-permute-start | bytes 2949128 | tf_op jit(solution)/shard_map/ppermute | solution.py:24
  (88 other events, 154.2 us)
where the time goes:
time: 400 us; the launch traced here: 394 us
  local copies, waits for them, and re-layouts  113 us (28%)
  waiting for transfers between devices  104 us (26%)
  other arithmetic  104 us (26%)
  blocking collectives  33.8 us (8%)
  starting transfers between devices  24.6 us (6%)
  matrix products  11.2 us (3%)
    ppermute x3, waiting for transfers between devices, extended_2(): lax.ppermute(tail, axis, [(i, (i + 1) % count) for i in range(count)])  78.6 us
    slice x48, local copies, waits for them, and re-layouts, residual(): jnp.pad(component, ((0, 0), (0, 0), (0, 0), (2, 2)), mode='edge')  44.3 us
    sub x20, other arithmetic, divergence(): 0.5 * (left_flux[member] + right_flux[member])  43.9 us
    all_to_all x1, blocking collectives, body(): lax.all_to_all(change_freq, 'inst', split_axis=0, concat_axis=2, tiled=True)  33.8 us
    unnamed x212, local copies, waits for them, and re-layouts  26.6 us
    reshape x20, local copies, waits for them, and re-layouts, residual(): jnp.pad(component, ((0, 0), (0, 0), (0, 0), (2, 2)), mode='edge')  17.8 us
    all_to_all x1, waiting for transfers between devices, body(): lax.all_to_all(second_sweep, 'inst', split_axis=2, concat_axis=0, tiled=T...  16.2 us
    concatenate x10, other arithmetic, residual(): jnp.pad(component, ((0, 0), (0, 0), (0, 0), (2, 2)), mode='edge')  14.2 us
  transfers between devices with their start and end apart: 8, of which 7 were waited for; matrix products, arithmetic and copies ran while one was open for 25% of the time, Pallas kernels for 0%

commit v1 on v0

--- a/solution.py
+++ b/solution.py
@@ -168,7 +168,12 @@
     second_sweep = residual(segmented_ext)
     state_freq, residual_freq = (
         lax.all_to_all(state, "inst", split_axis=2, concat_axis=0, tiled=True),
-        lax.all_to_all(second_sweep, "inst", split_axis=2, concat_axis=0, tiled=True),
+        jnp.concatenate(
+            lax.all_to_all(
+                jnp.stack(jnp.split(second_sweep, lax.axis_size("inst"), axis=2)), "inst", 0, 0
+            ),
+            axis=0,
+        ),
     )
     forward, inverse = transform_tables(NT)
     layout = residual_freq.shape

time: 400 us -> 384 us (0.960)
  other arithmetic: 104 us -> 96 us
  local copies, waits for them, and re-layouts: 113 us -> 106 us
    reshape x20, local copies, waits for them, and re-layouts: 17.8 us -> 10.1 us  [residual(): jnp.pad(component, ((0, 0), (0, 0), (0, 0), (2, 2)), mode='edge')]
    slice x48, local copies, waits for them, and re-layouts: 44.3 us -> 37.7 us  [residual(): jnp.pad(component, ((0, 0), (0, 0), (0, 0), (2, 2)), mode='edge')]
    sub x28, other arithmetic: 10.2 us -> 5.04 us  [divergence(): take_part(component, 1, extent - 1, along)]
    sub x20, other arithmetic: 43.9 us -> 38.9 us  [divergence(): 0.5 * (left_flux[member] + right_flux[member])]
    slice x10, local copies, waits for them, and re-layouts: 0.71 us -> 4.9 us  [residual(): inner = [component[:, :, 2:-2, :] for component in states]]
    unnamed x212 -> x170, local copies, waits for them, and re-layouts: 26.6 us -> 25.5 us
  transfers between devices with their start and end apart: 8 -> 8, of which waited for: 7 -> 7; matrix products, arithmetic and copies ran while one was open for 25% -> 22% of each run, Pallas kernels for 0% -> 0%
where the time goes in v1:
time: 384 us; the launch traced here: 378 us
  local copies, waits for them, and re-layouts  106 us (28%)
  waiting for transfers between devices  104 us (27%)
  other arithmetic  96 us (25%)
  blocking collectives  33.8 us (9%)
  starting transfers between devices  25.1 us (7%)
  matrix products  11 us (3%)
    ppermute x3, waiting for transfers between devices, extended_2(): lax.ppermute(tail, axis, [(i, (i + 1) % count) for i in range(count)])  77.8 us
    sub x20, other arithmetic, divergence(): 0.5 * (left_flux[member] + right_flux[member])  38.9 us
    slice x48, local copies, waits for them, and re-layouts, residual(): jnp.pad(component, ((0, 0), (0, 0), (0, 0), (2, 2)), mode='edge')  37.7 us
    all_to_all x1, blocking collectives, body(): lax.all_to_all(change_freq, 'inst', split_axis=0, concat_axis=2, tiled=True)  33.8 us
    unnamed x170, local copies, waits for them, and re-layouts  25.5 us
    all_to_all x1, waiting for transfers between devices, body(): lax.all_to_all(jnp.stack(jnp.split(second_sweep, lax.axis_size('inst'), a...  16.3 us
    concatenate x10, other arithmetic, residual(): jnp.pad(component, ((0, 0), (0, 0), (0, 0), (2, 2)), mode='edge')  14.2 us
    add x30, other arithmetic, limited(): jnp.maximum(0.0, jnp.minimum(lower, upper))  13.5 us
  transfers between devices with their start and end apart: 8, of which 7 were waited for; matrix products, arithmetic and copies ran while one was open for 22% of the time, Pallas kernels for 0%

profile of v1, /device:TPU:0, one launch (start us, length us, event | category | flops | bytes accessed | tf_op | source)
XLA Modules:
  0.0 377.7 jit_solution(6455743470994783318)
XLA Ops:
  0.0 3.2 fusion.217
  3.2 3.0 collective-permute-start
  6.2 3.1 collective-permute-start.1
  9.3 24.9 %collective-permute-done = f32[4,5,16,2,256]{4,3,0,2,1:T(2,128)S(1)} collective-permute-done((f32[4,5,16,2,256]{4,3,0,2,1:T(2,128)S(1)}, f32[4,5,16,2,256]{4,3,0,2,1:T(2,128)S(1)}, u32[]{:S(2)}, u32[]{:S(2)}) %collective-permute-start) | collective-permute-done | bytes 655392 | tf_op jit(solution)/shard_map/ppermute | solution.py:22
  93.8 4.1 %multiply_subtract_fusion.16 = (f32[4,16,8,257]{3,2,0,1:T(8,128)S(1)}, f32[4,16,8,257]{3,2,0,1:T(8,128)S(1)}, f32[4,16,8,257]{3,2,0,1:T(8,128)S(1)}, f32[4,16,8,257]{3,2,0,1:T(8,128)S(1)}, f32[4,16,8,257]{3,2,0,1:T(8,128)S(1)}) fusion(f32[4,16,8,258]{3,2,0,1:T(8,128)S(1)} %copy-done.21, f32[4,16,8,256]{3,2,0,1:T(8,128)S(1)} %copy-done.28, ...), kind=kLoop, calls=%fused_computation.255 | loop fusion | flops 8816128 | bytes 10557440 | tf_op jit(solution)/shard_map/sub | solution.py:104
  107.2 3.5 multiply_subtract_fusion.6
  120.6 4.4 %collective-permute-start.3 = (f32[4,5,16,2,256]{4,3,0,2,1:T(2,128)}, f32[4,5,16,2,256]{4,3,0,2,1:T(2,128)}, u32[]{:S(2)}, u32[]{:S(2)}) collective-permute-start(f32[4,5,16,2,256]{4,3,0,2,1:T(2,128)} %get-tuple-element.78), channel_id=1, source_target_pairs={{1,0},{2,1},{3,2},{4,3},{5,4},{6,5},{7,6},{0,7},{9,8},{10,9},{11,1... | collective-permute-start | bytes 1966088 | tf_op jit(solution)/shard_map/ppermute | solution.py:24
  126.8 5.3 %all-to-all-start.1 = ((f32[4,5,16,8,256]{4,3,1,0,2:T(8,128)}), f32[4,5,16,8,256]{4,3,1,0,2:T(8,128)}, u32[]{:S(2)}, u32[]{:S(2)}) async-start(f32[4,5,16,8,256]{4,3,1,0,2:T(8,128)} %copy.117), calls=%async_computation.1 | async-start | bytes 5242880 | tf_op jit(solution)/shard_map/all_to_all | solution.py:170
  132.1 16.0 %collective-permute-done.2 = f32[4,5,16,2,256]{4,3,0,2,1:T(2,128)} collective-permute-done((f32[4,5,16,2,256]{4,3,0,2,1:T(2,128)}, f32[4,5,16,2,256]{4,3,0,2,1:T(2,128)}, u32[]{:S(2)}, u32[]{:S(2)}) %collective-permute-start.2) | collective-permute-done | bytes 655392 | tf_op jit(solution)/shard_map/ppermute | solution.py:22
  148.1 3.9 %collective-permute-done.3 = f32[4,5,16,2,256]{4,3,0,2,1:T(2,128)} collective-permute-done((f32[4,5,16,2,256]{4,3,0,2,1:T(2,128)}, f32[4,5,16,2,256]{4,3,0,2,1:T(2,128)}, u32[]{:S(2)}, u32[]{:S(2)}) %collective-permute-start.3) | collective-permute-done | bytes 655392 | tf_op jit(solution)/shard_map/ppermute | solution.py:24
  199.5 4.1 %multiply_subtract_fusion.11 = (f32[4,16,8,257]{3,2,0,1:T(8,128)S(1)}, f32[4,16,8,257]{3,2,0,1:T(8,128)S(1)}, f32[4,16,8,257]{3,2,0,1:T(8,128)S(1)}, f32[4,16,8,257]{3,2,0,1:T(8,128)S(1)}, f32[4,16,8,257]{3,2,0,1:T(8,128)S(1)}) fusion(f32[4,16,8,258]{3,2,0,1:T(8,128)S(1)} %minimum_add_fusion.11, f32[4,16,8,256]{3,2,0,1:T(8,128)S(1)} %copy-done.26, ...), kind=kLoop, calls=%fused_computation.244 | loop fusion | flops 8816128 | bytes 10557440 | tf_op jit(solution)/shard_map/sub | solution.py:104
  216.7 3.5 multiply_subtract_fusion.1
  226.7 3.8 %all-to-all-start = ((f32[4,4,5,4,8,256]{5,4,1,3,2,0:T(8,128)}), f32[4,4,5,4,8,256]{5,4,1,3,2,0:T(8,128)S(1)}, u32[]{:S(2)}, u32[]{:S(2)}) async-start(f32[4,4,5,4,8,256]{5,4,1,3,2,0:T(8,128)} %pad_maximum_fusion.3), calls=%async_computation | async-start | bytes 5242880 | tf_op jit(solution)/shard_map/all_to_all | solution.py:172
  230.7 3.6 copy.147
  234.3 3.0 reshape.404
  239.9 3.7 fusion.22
  245.5 16.3 %all-to-all-done = f32[4,4,5,4,8,256]{5,4,1,3,2,0:T(8,128)S(1)} async-done(((f32[4,4,5,4,8,256]{5,4,1,3,2,0:T(8,128)}), f32[4,4,5,4,8,256]{5,4,1,3,2,0:T(8,128)S(1)}, u32[]{:S(2)}, u32[]{:S(2)}) %all-to-all-start) | async-done | bytes 2621472 | tf_op jit(solution)/shard_map/all_to_all | solution.py:172
  267.3 3.7 fusion.21
  271.4 5.1 %collective-permute-start.5 = (f32[8,2,5,4,3,256]{5,0,4,3,2,1:T(8,128)S(1)}, f32[8,2,5,4,3,256]{5,0,4,3,2,1:T(8,128)S(1)}, u32[]{:S(2)}, u32[]{:S(2)}) collective-permute-start(f32[8,2,5,4,3,256]{5,0,4,3,2,1:T(8,128)S(1)} %get-tuple-element.72), channel_id=1, source_target_pairs={{1,0},{2,1},{3,2},{4,3},{5,4},{6,5},{7,6},{0,7},{9,8},{10,9},{11,1... | collective-permute-start | bytes 2949128 | tf_op jit(solution)/shard_map/ppermute | solution.py:24
  276.5 36.9 %collective-permute-done.4 = f32[8,2,5,4,3,256]{5,0,4,3,2,1:T(8,128)S(1)} collective-permute-done((f32[8,2,5,4,3,256]{5,0,4,3,2,1:T(8,128)S(1)}, f32[8,2,5,4,3,256]{5,0,4,3,2,1:T(8,128)S(1)}, u32[]{:S(2)}, u32[]{:S(2)}) %collective-permute-start.4) | collective-permute-done | bytes 983072 | tf_op jit(solution)/shard_map/ppermute | solution.py:22
  313.4 3.5 collective-permute-done.5
  331.0 3.2 reshape.405
  336.7 3.6 fusion.26
  341.9 33.8 %all_to_all.38 = f32[16,5,4,8,256]{4,3,2,1,0:T(8,128)S(1)} all-to-all(f32[16,5,4,8,256]{4,3,2,1,0:T(8,128)S(1)} %copy.122), channel_id=1, replica_groups=mesh['inst'=4,'blk'=8] {'inst'}, dimensions={0} | all-to-all | bytes 5242880 | tf_op jit(solution)/shard_map/all_to_all | solution.py:200
  (421 shorter events, 176.1 us)
Async XLA Ops:
  0.0 36.5 %copy-start.15 = (f32[4,5,16,8,256]{4,3,2,1,0:T(8,128)S(1)}, f32[4,5,16,8,256]{4,3,2,1,0:T(8,128)}, u32[]{:S(2)}) copy-start(f32[4,5,16,8,256]{4,3,2,1,0:T(8,128)} %param.2) | copy-start | bytes 7864324
  3.2 31.1 %collective-permute-start = (f32[4,5,16,2,256]{4,3,0,2,1:T(2,128)S(1)}, f32[4,5,16,2,256]{4,3,0,2,1:T(2,128)S(1)}, u32[]{:S(2)}, u32[]{:S(2)}) collective-permute-start(f32[4,5,16,2,256]{4,3,0,2,1:T(2,128)S(1)} %get-tuple-element.79), channel_id=1, source_target_pairs={{0,1},{1,2},{2,3},{3,4},{4,5},{5,6},{6,7},{7,0},{8,9},{9,10},{10,1... | collective-permute-start | bytes 1966088 | tf_op jit(solution)/shard_map/ppermute | solution.py:22
  6.2 30.2 %collective-permute-start.1 = (f32[4,5,16,2,256]{4,3,0,2,1:T(2,128)S(1)}, f32[4,5,16,2,256]{4,3,0,2,1:T(2,128)S(1)}, u32[]{:S(2)}, u32[]{:S(2)}) collective-permute-start(f32[4,5,16,2,256]{4,3,0,2,1:T(2,128)S(1)} %get-tuple-element.80), channel_id=1, source_target_pairs={{1,0},{2,1},{3,2},{4,3},{5,4},{6,5},{7,6},{0,7},{9,8},{10,9},{11,1... | collective-permute-start | bytes 1966088 | tf_op jit(solution)/shard_map/ppermute | solution.py:24
  38.5 8.8 %copy-start.7 = (f32[4,16,12,256]{3,2,0,1:T(8,128)}, f32[4,16,12,256]{3,2,0,1:T(8,128)S(1)}, u32[]{:S(2)}) copy-start(f32[4,16,12,256]{3,2,0,1:T(8,128)S(1)} %get-tuple-element.45) | copy-start | bytes 2359300
  38.6 4.3 %copy-start.24 = (f32[4,16,8,256]{3,2,0,1:T(8,128)}, f32[4,16,8,256]{3,2,0,1:T(8,128)S(1)}, u32[]{:S(2)}) copy-start(f32[4,16,8,256]{3,2,0,1:T(8,128)S(1)} %slice.1936) | copy-start | bytes 1572868
  38.7 5.8 %copy-start.17 = (f32[4,16,8,256]{3,2,0,1:T(8,128)}, f32[4,16,8,256]{3,2,0,1:T(8,128)S(1)}, u32[]{:S(2)}) copy-start(f32[4,16,8,256]{3,2,0,1:T(8,128)S(1)} %slice.1978) | copy-start | bytes 1572868
  38.8 5.7 %copy-start.3 = (f32[4,16,8,256]{3,2,0,1:T(8,128)}, f32[4,16,8,256]{3,2,0,1:T(8,128)S(1)}, u32[]{:S(2)}) copy-start(f32[4,16,8,256]{3,2,0,1:T(8,128)S(1)} %slice.1892) | copy-start | bytes 1572868
  39.0 9.5 %copy-start.13 = (f32[4,16,12,256]{3,2,0,1:T(8,128)}, f32[4,16,12,256]{3,2,0,1:T(8,128)S(1)}, u32[]{:S(2)}) copy-start(f32[4,16,12,256]{3,2,0,1:T(8,128)S(1)} %slice_bitcast_fusion.9) | copy-start | bytes 2359300
  39.4 5.1 %copy-start.5 = (f32[4,18,8,256]{3,2,0,1:T(8,128)}, f32[4,18,8,256]{3,2,0,1:T(8,128)S(1)}, u32[]{:S(2)}) copy-start(f32[4,18,8,256]{3,2,0,1:T(8,128)S(1)} %minimum_add_fusion.27) | copy-start | bytes 1769476
  54.0 2.9 copy-start.36
  88.1 4.1 %copy-start.61 = (f32[4,16,8,2]{3,2,0,1:T(8,128)S(1)}, f32[4,16,8,2]{3,2,0,1:T(8,128)}, u32[]{:S(2)}) copy-start(f32[4,16,8,2]{3,2,0,1:T(8,128)} %copy-done.60) | copy-start | bytes 12292
  89.0 3.2 copy-start.59
  120.3 27.8 %collective-permute-start.2 = (f32[4,5,16,2,256]{4,3,0,2,1:T(2,128)}, f32[4,5,16,2,256]{4,3,0,2,1:T(2,128)}, u32[]{:S(2)}, u32[]{:S(2)}) collective-permute-start(f32[4,5,16,2,256]{4,3,0,2,1:T(2,128)} %get-tuple-element.77), channel_id=1, source_target_pairs={{0,1},{1,2},{2,3},{3,4},{4,5},{5,6},{6,7},{7,0},{8,9},{9,10},{10,1... | collective-permute-start | bytes 1966088 | tf_op jit(solution)/shard_map/ppermute | solution.py:22
  120.6 31.4 %collective-permute-start.3 = (f32[4,5,16,2,256]{4,3,0,2,1:T(2,128)}, f32[4,5,16,2,256]{4,3,0,2,1:T(2,128)}, u32[]{:S(2)}, u32[]{:S(2)}) collective-permute-start(f32[4,5,16,2,256]{4,3,0,2,1:T(2,128)} %get-tuple-element.78), channel_id=1, source_target_pairs={{1,0},{2,1},{3,2},{4,3},{5,4},{6,5},{7,6},{0,7},{9,8},{10,9},{11,1... | collective-permute-start | bytes 1966088 | tf_op jit(solution)/shard_map/ppermute | solution.py:24
  126.8 25.2 %copy-start.30 = (f32[4,5,16,8,256]{4,3,0,2,1:T(8,128)S(1)}, f32[4,5,16,8,256]{4,3,0,2,1:T(8,128)}, u32[]{:S(2)}) copy-start(f32[4,5,16,8,256]{4,3,0,2,1:T(8,128)} %copy-done.29) | copy-start | bytes 7864324
  126.8 99.9 %all-to-all-start.1 = ((f32[4,5,16,8,256]{4,3,1,0,2:T(8,128)}), f32[4,5,16,8,256]{4,3,1,0,2:T(8,128)}, u32[]{:S(2)}, u32[]{:S(2)}) async-start(f32[4,5,16,8,256]{4,3,1,0,2:T(8,128)} %copy.117), calls=%async_computation.1 | async-start | bytes 5242880 | tf_op jit(solution)/shard_map/all_to_all | solution.py:170
  154.4 8.2 %copy-start.11 = (f32[4,16,12,256]{3,2,0,1:T(8,128)}, f32[4,16,12,256]{3,2,0,1:T(8,128)S(1)}, u32[]{:S(2)}) copy-start(f32[4,16,12,256]{3,2,0,1:T(8,128)S(1)} %slice_bitcast_fusion.4) | copy-start | bytes 2359300
  157.0 8.2 %copy-start.9 = (f32[4,16,12,256]{3,2,0,1:T(8,128)}, f32[4,16,12,256]{3,2,0,1:T(8,128)S(1)}, u32[]{:S(2)}) copy-start(f32[4,16,12,256]{3,2,0,1:T(8,128)S(1)} %get-tuple-element.25) | copy-start | bytes 2359300
  182.9 3.0 copy-start.34
  195.4 2.5 copy-start.69
  226.7 3.8 %copy-start.82 = (s32[7]{0:T(128)S(1)}, s32[7]{0:T(128)}, u32[]{:S(2)}) copy-start(s32[7]{0:T(128)} %param.3) | copy-start | bytes 88
  226.7 35.0 %all-to-all-start = ((f32[4,4,5,4,8,256]{5,4,1,3,2,0:T(8,128)}), f32[4,4,5,4,8,256]{5,4,1,3,2,0:T(8,128)S(1)}, u32[]{:S(2)}, u32[]{:S(2)}) async-start(f32[4,4,5,4,8,256]{5,4,1,3,2,0:T(8,128)} %pad_maximum_fusion.3), calls=%async_computation | async-start | bytes 5242880 | tf_op jit(solution)/shard_map/all_to_all | solution.py:172
  271.3 42.1 %collective-permute-start.4 = (f32[8,2,5,4,3,256]{5,0,4,3,2,1:T(8,128)S(1)}, f32[8,2,5,4,3,256]{5,0,4,3,2,1:T(8,128)S(1)}, u32[]{:S(2)}, u32[]{:S(2)}) collective-permute-start(f32[8,2,5,4,3,256]{5,0,4,3,2,1:T(8,128)S(1)} %get-tuple-element.71), channel_id=1, source_target_pairs={{0,1},{1,2},{2,3},{3,4},{4,5},{5,6},{6,7},{7,0},{8,9},{9,10},{10,1... | collective-permute-start | bytes 2949128 | tf_op jit(solution)/shard_map/ppermute | solution.py:22
  271.4 45.5 %collective-permute-start.5 = (f32[8,2,5,4,3,256]{5,0,4,3,2,1:T(8,128)S(1)}, f32[8,2,5,4,3,256]{5,0,4,3,2,1:T(8,128)S(1)}, u32[]{:S(2)}, u32[]{:S(2)}) collective-permute-start(f32[8,2,5,4,3,256]{5,0,4,3,2,1:T(8,128)S(1)} %get-tuple-element.72), channel_id=1, source_target_pairs={{1,0},{2,1},{3,2},{4,3},{5,4},{6,5},{7,6},{0,7},{9,8},{10,9},{11,1... | collective-permute-start | bytes 2949128 | tf_op jit(solution)/shard_map/ppermute | solution.py:24
  (67 other events, 96.0 us)
